TPU v7x, 512 devices: a whole 4x8x8 slice. The times are simulated.
512 devices in a mesh: grp: 8 (over x, y_hi), blk: 64 (over z, y_lo, core).
Axes of the slice: x: 4, y: 8 (y_hi: 2, y_lo: 4; y = y_hi * 4 + y_lo), z: 8, core: 2. Of those that a mesh axis runs over, the one named last changes fastest.
Arguments:
- sensors: float32 [3, 131072], P(None, 'blk'), may hold values from 0 to 1
- sources: bfloat16 [3, 1048576], P(None, ('grp', 'blk')), may hold values from 0 to 1
- weights: bfloat16 [1048576], P(('grp', 'blk')), may hold values from 0.5 to 2
- probes: bfloat16 [1048576, 128], P(('grp', 'blk')), may hold values from -6 to 6
Outputs:
- response: float32 [128, 131072], P('grp', 'blk')
All inputs are finite; a program needn't handle non-finite values.
Results may differ from a plain program's by a relative error of at most 0.01.
Values may be sent and summed in bfloat16 or wider, within the bound.
A program may use at most 64 MiB of HBM per device.

v0:
```python
import functools
import math

import jax
import jax.numpy as jnp
from jax import lax
from jax.experimental import pallas as pl
from jax.experimental.pallas import tpu as pltpu
from jax.sharding import PartitionSpec as P

STEPS = 6
EPS = 0.0025
BF, F32 = jnp.bfloat16, jnp.float32


def pieces(v):
    hi = v.astype(BF).astype(F32)
    mid = (v - hi).astype(BF).astype(F32)
    return [hi, mid, v - hi - mid]


def squared(v):
    return v[0:1] * v[0:1] + v[1:2] * v[1:2] + v[2:3] * v[2:3]


def kernel(
    groups, blocks, sens, src, wgt, prb, out, prb_t, lhs, rhs, ker_a, ker_b, sens_in, work, inbox, buf_a, buf_b, buf_c, buf_d, rcv,
    sens_send, sens_recv, core_send, core_recv, a_send, a_recv, b_send, b_recv, c_send, c_recv, d_send, d_recv, f_send, f_recv,
):
    sources, sensors = src.shape[1], sens.shape[1]
    half, chunk = sensors // 2, sensors // 4
    nx = groups // 2
    grp, blk = lax.axis_index("grp"), lax.axis_index("blk")
    x, yh = grp // 2, grp % 2
    core = blk % 2
    other = grp + 1 - 2 * yh
    at = lambda offset: (blk + offset + blocks) % blocks
    x_next = ((x + 1) % nx) * 2 + yh
    x_prev = ((x + nx - 1) % nx) * 2 + yh
    peer = blk + 1 - 2 * core

    barrier = pltpu.get_barrier_semaphore()
    near = [(grp, at(o)) for o in range(-STEPS + 1, STEPS) if o != 0]
    near += [(other, at(o)) for o in range(-STEPS + 1, STEPS)]
    near += [(x_next, blk), (x_prev, blk)]
    for device in near:
        pl.semaphore_signal(barrier, inc=1, device_id=device, device_id_type=pl.DeviceIdType.MESH)

    def copy(source, target, send, recv, device):
        return pltpu.make_async_remote_copy(source, target, send, recv, device_id=device, device_id_type=pl.DeviceIdType.MESH)

    started = []

    def send(*args):
        started.append(copy(*args))
        started[-1].start()

    scale = 1.0 / math.sqrt(STEPS * sources * groups)
    prb_t[...] = (jnp.transpose(prb[...].astype(F32)) * (wgt[...].astype(F32) * scale)).astype(BF)
    place = src[...].astype(F32)
    ones = jnp.ones((1, sources), F32)
    rows = [-2.0 * place] * 3 + [ones] * 3 + pieces(squared(place)) + [jnp.zeros((113, sources), F32)]
    lhs[...] = jnp.transpose(jnp.concatenate(rows, axis=0)).astype(BF)
    rhs[...] = jnp.zeros_like(rhs)
    sens_in[0] = sens[...]

    def offset_of(step):
        if step == 0:
            return 0
        if step == 1:
            return jnp.where(core == 0, 1, STEPS - 1)
        return 7 - step - core

    def piece_of(step, j):
        if step < 2:
            alone = core == step
            return jnp.where(alone, j, 3 - j)
        return 2 * step + 1 - j

    def prepare(step, j):
        columns = jnp.where(core == j, half, 0)
        where = sens_in[offset_of(step), :, pl.ds(pl.multiple_of(columns, 128), half)]
        parts = pieces(where)
        ones_row = jnp.ones((3, half), F32)
        rows = parts + pieces(squared(where) + EPS) + [ones_row, jnp.zeros((1, half), F32)]
        rhs[j, 0:16] = jnp.concatenate(rows, axis=0).astype(BF)

    def distances(n):
        ker = (ker_a, ker_b)[n % 2]
        dist = jnp.dot(lhs[...], rhs[(n % 4) // 2, :, pl.ds((n % 2) * chunk, chunk)], preferred_element_type=F32)
        ker[...] = lax.rsqrt(dist).astype(BF)

    def apply(n):
        ker = (ker_a, ker_b)[n % 2]
        part = jnp.dot(prb_t[...], ker[...], preferred_element_type=F32)
        part = part.astype(BF).reshape(groups, part.shape[0] // groups, chunk)
        work[piece_of(n // 4, (n % 4) // 2), :, :, pl.ds((n % 2) * chunk, chunk)] = part

    def unit_kk(u):
        return 6 * core if u < 2 else (1, 5, 4, 3, 2)[u - 2]

    def unit_at(u):
        return u if u < 2 else 2 * u - 2

    def unit_half(u):
        return core if u > 0 else 1 - core

    far, fore, back = (x + 2) % nx * 2, (x + 1) % nx * 2, (x + nx - 1) % nx * 2

    def stage1(u):
        w = unit_at(u)
        if u >= 2:
            s = u - 2
            copy(work.at[w], inbox.at[s], core_send.at[s], core_recv.at[s], (grp, peer)).wait_recv()
            work[w] = (work[w].astype(F32) + inbox[s].astype(F32)).astype(BF)
        send(work.at[w, far], buf_a.at[u], a_send.at[u], a_recv.at[u], (x_next, blk))
        send(work.at[w, far + 1], buf_b.at[u], b_send.at[u], b_recv.at[u], (x_prev, blk))

    def stage2(u):
        w = unit_at(u)
        copy(buf_a.at[u], buf_a.at[u], a_send.at[u], a_recv.at[u], (x_prev, blk)).wait_recv()
        work[w, fore] = (work[w, fore].astype(F32) + buf_a[u].astype(F32)).astype(BF)
        send(work.at[w, pl.ds(fore, 2)], buf_c.at[u], c_send.at[u], c_recv.at[u], (x_next, blk))
        copy(buf_b.at[u], buf_b.at[u], b_send.at[u], b_recv.at[u], (x_next, blk)).wait_recv()
        work[w, back + 1] = (work[w, back + 1].astype(F32) + buf_b[u].astype(F32)).astype(BF)
        send(work.at[w, pl.ds(back, 2)], buf_d.at[u], d_send.at[u], d_recv.at[u], (x_prev, blk))

    def final(u, away):
        w, kk, h = unit_at(u), unit_kk(u), unit_half(u)
        row = grp if away == 0 else other
        device = (row, at(kk - core))
        return copy(work.at[w, row], rcv.at[kk // 2, away, h], f_send.at[u, away], f_recv.at[kk // 2, away, h], device)

    def stage3(u):
        w, kk, h = unit_at(u), unit_kk(u), unit_half(u)
        copy(buf_c.at[u], buf_c.at[u], c_send.at[u], c_recv.at[u], (x_prev, blk)).wait_recv()
        copy(buf_d.at[u], buf_d.at[u], d_send.at[u], d_recv.at[u], (x_next, blk)).wait_recv()
        own = pl.ds(x * 2, 2)
        work[w, own] = (work[w, own].astype(F32) + buf_c[u].astype(F32) + buf_d[u].astype(F32)).astype(BF)
        final(u, 1).start()
        if u < 3:
            mine = core == (0 if u < 2 else 1)

            @pl.when(mine)
            def _():
                rcv[0, 0, h] = work[w, grp]

            @pl.when(jnp.logical_not(mine))
            def _():
                final(u, 0).start()
        else:
            final(u, 0).start()

    def finish_final(u):
        final(u, 1).wait_send()
        if u < 3:

            @pl.when(core != (0 if u < 2 else 1))
            def _():
                final(u, 0).wait_send()
        else:
            final(u, 0).wait_send()

    batches = {1: (0, 1, 2), 2: (3,), 3: (4,), 4: (5,), 5: (6,)}
    total = 4 * STEPS
    prepare(0, 0)
    distances(0)
    for n in range(total):
        step, j, last = n // 4, (n % 4) // 2, n % 2 == 1
        if n == 1:
            pl.semaphore_wait(barrier, len(near))
            for o in range(1, STEPS):
                send(sens, sens_in.at[o], sens_send.at[o - 1], sens_recv.at[o - 1], (grp, at(-o)))
        if n + 1 < total:
            if n + 1 == 4:
                for o in range(1, STEPS):
                    copy(sens, sens_in.at[o], sens_send.at[o - 1], sens_recv.at[o - 1], (grp, at(o))).wait_recv()
            if (n + 1) % 2 == 0:
                prepare((n + 1) // 4, ((n + 1) % 4) // 2)
            distances(n + 1)
        apply(n)
        if last and step >= 1:
            if j == 0:
                s = step - 1
                send(work.at[3 + 2 * s], inbox.at[s], core_send.at[s], core_recv.at[s], (grp, peer))
            else:
                for u in batches[step]:
                    stage1(u)
                for u in batches.get(step - 1, ()):
                    stage2(u)
                for u in batches.get(step - 2, ()):
                    stage3(u)
    stage2(6)
    stage3(5)
    stage3(6)

    sums = [None, None]
    for q in range(3):
        for away in range(2):
            for h in range(2):
                slot = rcv.at[q, away, h]

                def wait(slot=slot, index=(q, away, h)):
                    copy(slot, slot, f_send.at[0, 0], f_recv.at[index], (other, blk)).wait_recv()

                if q > 0 or away > 0:
                    wait()
                elif h == 0:
                    pl.when(core == 1)(wait)
    for h in range(2):
        for q in range(3):
            for away in range(2):
                term = rcv[q, away, h].astype(F32)
                sums[h] = term if sums[h] is None else sums[h] + term
        out[:, h * half : (h + 1) * half] = sums[h]

    @pl.when(core == 0)
    def _():
        for h in range(2):
            for away in range(2):
                copy(rcv.at[3, away, h], rcv.at[3, away, h], f_send.at[0, 0], f_recv.at[3, away, h], (other, blk)).wait_recv()
            out[:, h * half : (h + 1) * half] = sums[h] + (rcv[3, 0, h].astype(F32) + rcv[3, 1, h].astype(F32))

    for sent in started:
        sent.wait_send()
    for u in range(7):
        finish_final(u)


def solution(mesh):
    groups, blocks = mesh.shape["grp"], mesh.shape["blk"]

    def step(sensors, sources, weights, probes):
        (columns, probe), count = (sensors.shape[1], probes.shape[1]), probes.shape[0]
        rows, half, chunk = probe // groups, columns // 2, columns // 4
        vmem = pl.BlockSpec(memory_space=pltpu.VMEM)
        dma = pltpu.SemaphoreType.DMA
        return pl.pallas_call(
            functools.partial(kernel, groups, blocks),
            out_shape=jax.ShapeDtypeStruct((rows, columns), F32),
            in_specs=[vmem] * 4,
            out_specs=vmem,
            scratch_shapes=[
                pltpu.VMEM((probe, count), BF),
                pltpu.VMEM((count, 128), BF),
                pltpu.VMEM((2, 128, half), BF),
                pltpu.VMEM((count, chunk), BF),
                pltpu.VMEM((count, chunk), BF),
                pltpu.VMEM((STEPS, 3, columns), F32),
                pltpu.VMEM((12, groups, rows, half), BF),
                pltpu.VMEM((5, groups, rows, half), BF),
                pltpu.VMEM((7, rows, half), BF),
                pltpu.VMEM((7, rows, half), BF),
                pltpu.VMEM((7, 2, rows, half), BF),
                pltpu.VMEM((7, 2, rows, half), BF),
                pltpu.VMEM((4, 2, 2, rows, half), BF),
            ]
            + [dma((n,)) for n in (5, 5, 5, 5, 7, 7, 7, 7, 7, 7, 7, 7)]
            + [dma((7, 2)), dma((4, 2, 2))],
            compiler_params=pltpu.CompilerParams(collective_id=0, has_side_effects=True, vmem_limit_bytes=48 * 2**20),
        )(sensors, sources, weights.reshape(1, -1), probes)

    in_specs = (P(None, "blk"), P(None, ("grp", "blk")), P(("grp", "blk")), P(("grp", "blk"), None))
    return jax.shard_map(step, mesh=mesh, in_specs=in_specs, out_specs=P("grp", "blk"), check_vma=False)
```

profile of v0, /device:TPU:1, one launch (start us, length us, event | category | flops | bytes accessed | tf_op | source)
XLA Modules:
  0.0 61.2 jit_solution(17774795027937488270)
XLA Ops:
  0.0 0.7 %reshape.3.wgt = bf16[1,2048]{1,0:T(2,128)(2,1)S(1)} reshape(bf16[2048]{0:T(1024)(128)(2,1)} %param.6) | data formatting | bytes 8192 | tf_op jit(solution)/shard_map/reshape | solution.py:261
  0.7 0.0 copy-start
  0.7 1.0 %copy-done = bf16[2048,128]{1,0:T(8,128)(2,1)S(1)} copy-done((bf16[2048,128]{1,0:T(8,128)(2,1)S(1)}, bf16[2048,128]{1,0:T(8,128)(2,1)}, u32[]{:S(2)}) %copy-start) | copy-done | bytes 524312
  1.7 0.0 copy-start.1
  1.7 0.8 %copy-done.1 = f32[3,2048]{1,0:T(4,128)S(1)} copy-done((f32[3,2048]{1,0:T(4,128)S(1)}, f32[3,2048]{1,0:T(4,128)}, u32[]{:S(2)}) %copy-start.1) | copy-done | bytes 24600
  2.5 0.0 copy-start.2
  2.5 0.7 %copy-done.2 = bf16[3,2048]{1,0:T(4,128)(2,1)S(1)} copy-done((bf16[3,2048]{1,0:T(4,128)(2,1)S(1)}, bf16[3,2048]{1,0:T(4,128)(2,1)}, u32[]{:S(2)}) %copy-start.2) | copy-done | bytes 12312
  3.2 57.4 %shard_map.46 = f32[16,2048]{1,0:T(8,128)S(1)} custom-call(f32[3,2048]{1,0:T(4,128)S(1)} %copy-done.1, bf16[3,2048]{1,0:T(4,128)(2,1)S(1)} %copy-done.2, bf16[1,2048]{1,0:T(2,128)(2,1)S(1)} %reshape.3.wgt, bf16[2048,128]{1,0:T(8,128)(2,1)S(1)} %copy-done), custom_call_target="tpu_custom_call" | custom-call | tf_op jit(solution)/shard_map/pallas_call | solution.py:238
  60.6 0.7 %copy.6 = f32[16,2048]{1,0:T(8,128)} copy(f32[16,2048]{1,0:T(8,128)S(1)} %shard_map.46) | data formatting | bytes 262144
Async XLA Ops:
  0.7 1.0 %copy-start = (bf16[2048,128]{1,0:T(8,128)(2,1)S(1)}, bf16[2048,128]{1,0:T(8,128)(2,1)}, u32[]{:S(2)}) copy-start(bf16[2048,128]{1,0:T(8,128)(2,1)} %prb.1) | copy-start | bytes 1572868
  1.7 0.8 %copy-start.1 = (f32[3,2048]{1,0:T(4,128)S(1)}, f32[3,2048]{1,0:T(4,128)}, u32[]{:S(2)}) copy-start(f32[3,2048]{1,0:T(4,128)} %sens.1) | copy-start | bytes 73732
  2.5 0.7 %copy-start.2 = (bf16[3,2048]{1,0:T(4,128)(2,1)S(1)}, bf16[3,2048]{1,0:T(4,128)(2,1)}, u32[]{:S(2)}) copy-start(bf16[3,2048]{1,0:T(4,128)(2,1)} %src.1) | copy-start | bytes 36868
where the time goes:
time: 61.6 us; the launch traced here: 61.2 us
  Pallas kernels  57.4 us (93%)
  local copies, waits for them, and re-layouts  3.87 us (6%)
    pallas_call x1, Pallas kernels, step(): pl.pallas_call(functools.partial(kernel, groups, blocks), out_shape=jax.S...  57.4 us
    unnamed x7, local copies, waits for them, and re-layouts  3.17 us

commit v1 on v0

v1 whole, which is shorter than its diff:
```python
import functools
import math

import jax
import jax.numpy as jnp
from jax import lax
from jax.experimental import pallas as pl
from jax.experimental.pallas import tpu as pltpu
from jax.sharding import PartitionSpec as P

STEPS = 6
EPS = 0.0025
BF, F32 = jnp.bfloat16, jnp.float32
MESH = pl.DeviceIdType.MESH

ORDER = ((0, 0, 5, 5, 4, 4, 3, 3, 2, 2, 1, 1), (1, 1, 6, 6, 5, 5, 4, 4, 3, 3, 2, 2))
TILE = 256
ON_MXU = 256


def pieces(v):
    hi = v.astype(BF).astype(F32)
    mid = (v - hi).astype(BF).astype(F32)
    return [hi, mid, v - hi - mid]


def squared(v):
    return v[0:1] * v[0:1] + v[1:2] * v[1:2] + v[2:3] * v[2:3]


def kernel(
    groups, blocks, sens, src, wgt, prb, out, prb_in, src_in, wgt_in, prb_t, lhs, lanes, rhs, rows_of, ker_a, ker_b, sens_in, work,
    inbox, buf_a, buf_b, buf_c, buf_d, rcv, load, ready, sens_send, sens_recv, core_send, core_recv, a_send, a_recv, b_send, b_recv,
    c_send, c_recv, d_send, d_recv, f_send, f_recv,
):
    sources, sensors = src.shape[1], sens.shape[1]
    half, chunk = sensors // 2, sensors // 4
    nx = groups // 2
    grp, blk = lax.axis_index("grp"), lax.axis_index("blk")
    x, yh = grp // 2, grp % 2
    core = blk % 2
    other = grp + 1 - 2 * yh
    x_next = ((x + 1) % nx) * 2 + yh
    x_prev = ((x + nx - 1) % nx) * 2 + yh
    peer = blk + 1 - 2 * core

    def at(offset):
        return (blk + offset + blocks) % blocks

    def by_core(a, b):
        return a if a == b else jnp.where(core == 0, a, b)

    def signal(semaphore, device):
        pl.semaphore_signal(semaphore, inc=1, device_id=device, device_id_type=MESH)

    def copy(source, target, send, recv, device):
        return pltpu.make_async_remote_copy(source, target, send, recv, device_id=device, device_id_type=MESH)

    started = []

    def send(*args):
        started.append(copy(*args))
        started[-1].start()

    barrier = pltpu.get_barrier_semaphore()
    for o in range(1, STEPS):
        signal(barrier, (grp, at(-o)))
        pl.when(blk + o < blocks)(lambda o=o: signal(barrier, (grp, at(o))))
    for o in range(STEPS):
        signal(barrier, (other, at(-o)))
    for row in (x_next, x_prev):
        signal(barrier, (row, blk))
    expected = 3 * STEPS - jnp.maximum(STEPS - 1 - blk, 0)

    loads = [
        pltpu.make_async_copy(ref, target, load.at[i])
        for i, (ref, target) in enumerate(((src, src_in), (sens, sens_in.at[0]), (wgt, wgt_in), (prb, prb_in)))
    ]
    for step in loads:
        step.start()
    rhs[...] = jnp.zeros_like(rhs)

    loads[0].wait()
    place = src_in[...].astype(F32)
    rows = [-2.0 * place] * 3 + [jnp.ones((3, sources), F32)] + pieces(squared(place)) + [jnp.zeros((113, sources), F32)]
    lhs[...] = jnp.transpose(jnp.concatenate(rows, axis=0)).astype(BF)
    if ON_MXU < chunk:
        for i in range(3):
            lanes[i] = jnp.transpose(jnp.broadcast_to(place[i : i + 1], (128, sources))).astype(BF)
    loads[1].wait()
    loads[2].wait()
    scale = 1.0 / math.sqrt(STEPS * sources * groups)
    weight = wgt_in[...].astype(F32) * scale
    weight = jnp.concatenate([weight[i : i + 1] for i in range(weight.shape[0])], axis=1)
    loads[3].wait()
    prb_t[...] = (jnp.transpose(prb_in[...].astype(F32)) * weight).astype(BF)

    def turn(hs):
        return by_core(ORDER[0][hs], ORDER[1][hs]), hs % 2

    def slot_of(hs):
        kk0, kk1 = ORDER[0][hs], ORDER[1][hs]
        j = hs % 2
        return by_core(j if kk0 == 0 else 2 * kk0 + 1 - j, j if kk1 == 6 else 2 * kk1 + 1 - j)

    def prepare(hs):
        kk, j = turn(hs)
        columns = jnp.where(core == j, half, 0)
        where = sens_in[kk - core, :, pl.ds(pl.multiple_of(columns, 128), half)]
        parts = pieces(where)
        rows = parts + pieces(squared(where) + EPS) + [jnp.ones((3, half), F32), jnp.zeros((1, half), F32)]
        rhs[hs % 2, 0:16] = jnp.concatenate(rows, axis=0).astype(BF)
        rows_of[hs % 2] = jnp.concatenate([parts[0], where - parts[0], jnp.zeros((2, half), F32)], axis=0)

    def evaluate(n, k):
        ker, hs, first = (ker_a, ker_b)[n % 2], n // 2, (n % 2) * chunk
        span = pl.ds(k * TILE, TILE)
        dist = jnp.dot(lhs[span], rhs[hs % 2, :, pl.ds(first, ON_MXU)], preferred_element_type=F32)
        ker[span, 0:ON_MXU] = lax.rsqrt(dist).astype(BF)
        width = chunk - ON_MXU
        if width == 0:
            return
        near = [
            jnp.broadcast_to(rows_of[hs % 2, i : i + 1, pl.ds(first + ON_MXU, width)], (16, width)).astype(BF) for i in range(6)
        ]
        for r in range(k * TILE, (k + 1) * TILE, 16):
            total = None
            for i in range(3):
                delta = jnp.concatenate([lanes[i, r : r + 16]] * (width // 128), axis=1) - near[i] - near[3 + i]
                total = delta * delta if total is None else total + delta * delta
            ker[r : r + 16, ON_MXU:chunk] = lax.rsqrt(total + jnp.asarray(EPS, BF))

    def block(n):
        part = None
        for k in range(sources // TILE):
            if n + 1 < 4 * STEPS:
                evaluate(n + 1, k)
            if n >= 0:
                span = pl.ds(k * TILE, TILE)
                term = jnp.dot(prb_t[:, span], (ker_a, ker_b)[n % 2][span], preferred_element_type=F32)
                part = term if part is None else part + term
        if n >= 0:
            part = part.astype(BF).reshape(groups, part.shape[0] // groups, chunk)
            work[slot_of(n // 2), :, :, pl.ds((n % 2) * chunk, chunk)] = part

    def unit_kk(u):
        return by_core(*((0, 6), (0, 6), (5, 5), (4, 4), (3, 3), (2, 1), (1, 2))[u])

    def unit_at(u):
        return u if u < 2 else 2 * unit_kk(u)

    def unit_half(u):
        return core if u > 0 else 1 - core

    far, fore, back = (x + 2) % nx * 2, (x + 1) % nx * 2, (x + nx - 1) % nx * 2

    def to_peer(kk):
        return copy(work.at[2 * kk + 1], inbox.at[kk - 1], core_send.at[kk - 1], core_recv.at[kk - 1], (grp, peer))

    def stage1(u):
        w = unit_at(u)
        if u >= 2:
            kk = unit_kk(u)
            to_peer(kk).wait_recv()
            work[w] = (work[w].astype(F32) + inbox[kk - 1].astype(F32)).astype(BF)
        send(work.at[w, far], buf_a.at[u], a_send.at[u], a_recv.at[u], (x_next, blk))
        send(work.at[w, far + 1], buf_b.at[u], b_send.at[u], b_recv.at[u], (x_prev, blk))

    def stage2(u):
        w = unit_at(u)
        copy(buf_a.at[u], buf_a.at[u], a_send.at[u], a_recv.at[u], (x_prev, blk)).wait_recv()
        work[w, fore] = (work[w, fore].astype(F32) + buf_a[u].astype(F32)).astype(BF)
        send(work.at[w, pl.ds(fore, 2)], buf_c.at[u], c_send.at[u], c_recv.at[u], (x_next, blk))
        copy(buf_b.at[u], buf_b.at[u], b_send.at[u], b_recv.at[u], (x_next, blk)).wait_recv()
        work[w, back + 1] = (work[w, back + 1].astype(F32) + buf_b[u].astype(F32)).astype(BF)
        send(work.at[w, pl.ds(back, 2)], buf_d.at[u], d_send.at[u], d_recv.at[u], (x_prev, blk))

    def final(u, away):
        w, kk, h = unit_at(u), unit_kk(u), unit_half(u)
        row = grp if away == 0 else other
        device = (row, at(kk - core))
        return copy(work.at[w, row], rcv.at[kk // 2, away, h], f_send.at[u, away], f_recv.at[kk // 2, away, h], device)

    holder = {0: 0, 1: 0, 5: 1}

    def stage3(u):
        w, h = unit_at(u), unit_half(u)
        copy(buf_c.at[u], buf_c.at[u], c_send.at[u], c_recv.at[u], (x_prev, blk)).wait_recv()
        copy(buf_d.at[u], buf_d.at[u], d_send.at[u], d_recv.at[u], (x_next, blk)).wait_recv()
        own = pl.ds(x * 2, 2)
        work[w, own] = (work[w, own].astype(F32) + buf_c[u].astype(F32) + buf_d[u].astype(F32)).astype(BF)
        final(u, 1).start()
        if u in holder:

            @pl.when(core == holder[u])
            def _():
                rcv[0, 0, h] = work[w, grp]

            @pl.when(core != holder[u])
            def _():
                final(u, 0).start()
        else:
            final(u, 0).start()

    def sensors_to(o):
        copy(sens_in.at[0], sens_in.at[o], sens_send.at[o - 1], sens_recv.at[o - 1], (grp, at(-o))).start()

    def sensors_late(o):
        pl.semaphore_wait(ready.at[o - 1], 1)
        sensors_to(o)

    def meet():
        with jax.named_scope("barrier_wait"):
            pl.semaphore_wait(barrier, expected)
        for o in range(1, STEPS):
            pl.when(blk + o >= blocks)(lambda o=o: signal(ready.at[o - 1], (grp, at(o))))
            pl.when(blk >= o)(lambda o=o: sensors_to(o))

    def scoped(name, action, *args):
        with jax.named_scope(name):
            action(*args)

    def late():
        for o in range(1, STEPS):
            pl.when(blk < o)(functools.partial(sensors_late, o))

    def arrived():
        for o in range(1, STEPS):
            copy(sens_in.at[0], sens_in.at[o], sens_send.at[o - 1], sens_recv.at[o - 1], (grp, at(o))).wait_recv()

    def peer_send(kk0, kk1):
        if kk0 is None:
            pl.when(core == 1)(lambda: to_peer(kk1).start())
        elif kk1 is None:
            pl.when(core == 0)(lambda: to_peer(kk0).start())
        else:
            to_peer(by_core(kk0, kk1)).start()

    s1, s2, s3 = ((f"s{i + 1}", f) for i, f in enumerate((stage1, stage2, stage3)))
    after = {
        0: [("meet", meet)],
        1: [("core", peer_send, None, 1)],
        5: [("core", peer_send, 5, None)],
        7: [(*s1, 0), (*s1, 1)],
        9: [("core", peer_send, 4, 5)],
        11: [(*s1, 2), (*s2, 0), (*s2, 1)],
        13: [("core", peer_send, 3, 4)],
        15: [(*s1, 3), (*s2, 2), (*s3, 0), (*s3, 1)],
        17: [("core", peer_send, 2, 3)],
        19: [(*s1, 4), (*s2, 3), (*s3, 2)],
        21: [("core", peer_send, 1, 2), (*s3, 3)],
        22: [(*s1, 5), (*s2, 4)],
        23: [(*s1, 6), (*s2, 5), (*s2, 6), (*s3, 4), (*s3, 5), (*s3, 6)],
    }
    after.setdefault(9, []).append(("late", late))
    prepare(0)
    block(-1)
    for n in range(4 * STEPS):
        if n == 3:
            scoped("sens_wait", arrived)
        if n % 2 == 1 and n + 1 < 4 * STEPS:
            prepare((n + 1) // 2)
        block(n)
        for name, action, *args in after.get(n, ()):
            scoped("_".join([name, *map(str, args)]), action, *args)

    def landed(q, away, h):
        slot = rcv.at[q, away, h]
        copy(slot, slot, f_send.at[0, 0], f_recv.at[q, away, h], (other, blk)).wait_recv()

    def total(slots, h, base=None):
        for q, away in slots:
            term = rcv[q, away, h].astype(F32)
            base = term if base is None else base + term
        return base

    def gather():
        for h in range(2):
            pl.when(core == 0)(lambda h=h: [landed(3, 0, h), landed(3, 1, h)][0])
            for q in (2, 1):
                for away in range(2):
                    landed(q, away, h)
        pl.when(core == 1)(lambda: landed(0, 0, 0))
        for h in range(2):
            landed(0, 1, h)

    scoped("gather", gather)
    for h in range(2):
        part = total([(q, away) for q in range(3) for away in range(2)], h)
        far_part = total([(3, 0), (3, 1)], h)
        out[:, h * half : (h + 1) * half] = jnp.where(core == 0, part + far_part, part)

    for o in range(1, STEPS):
        copy(sens_in.at[0], sens_in.at[o], sens_send.at[o - 1], sens_recv.at[o - 1], (grp, at(-o))).wait_send()
    for kk in range(1, STEPS):
        to_peer(kk).wait_send()
    for sent in started:
        sent.wait_send()
    for u in range(7):
        final(u, 1).wait_send()
        if u in holder:
            pl.when(core != holder[u])(lambda u=u: final(u, 0).wait_send())
        else:
            final(u, 0).wait_send()


def solution(mesh):
    groups, blocks = mesh.shape["grp"], mesh.shape["blk"]

    def step(sensors, sources, weights, probes):
        (columns, probe), count = (sensors.shape[1], probes.shape[1]), probes.shape[0]
        rows, half, chunk = probe // groups, columns // 2, columns // 4
        dma = pltpu.SemaphoreType.DMA
        return pl.pallas_call(
            functools.partial(kernel, groups, blocks),
            out_shape=jax.ShapeDtypeStruct((rows, columns), F32),
            in_specs=[pl.BlockSpec(memory_space=pl.ANY)] * 4,
            out_specs=pl.BlockSpec(memory_space=pltpu.VMEM),
            scratch_shapes=[
                pltpu.VMEM((count, probe), BF),
                pltpu.VMEM((3, count), BF),
                pltpu.VMEM((count // 128, 128), BF),
                pltpu.VMEM((probe, count), BF),
                pltpu.VMEM((count, 128), BF),
                pltpu.VMEM((3, count, 128), BF),
                pltpu.VMEM((2, 128, half), BF),
                pltpu.VMEM((2, 8, half), F32),
                pltpu.VMEM((count, chunk), BF),
                pltpu.VMEM((count, chunk), BF),
                pltpu.VMEM((STEPS, 3, columns), F32),
                pltpu.VMEM((12, groups, rows, half), BF),
                pltpu.VMEM((5, groups, rows, half), BF),
                pltpu.VMEM((7, rows, half), BF),
                pltpu.VMEM((7, rows, half), BF),
                pltpu.VMEM((7, 2, rows, half), BF),
                pltpu.VMEM((7, 2, rows, half), BF),
                pltpu.VMEM((4, 2, 2, rows, half), BF),
                dma((4,)),
                pltpu.SemaphoreType.REGULAR((5,)),
            ]
            + [dma((n,)) for n in (5, 5, 5, 5, 7, 7, 7, 7, 7, 7, 7, 7)]
            + [dma((7, 2)), dma((4, 2, 2))],
            compiler_params=pltpu.CompilerParams(collective_id=0, has_side_effects=True, vmem_limit_bytes=63 * 2**20),
        )(sensors, sources, weights.reshape(-1, 128), probes)

    in_specs = (P(None, "blk"), P(None, ("grp", "blk")), P(("grp", "blk")), P(("grp", "blk"), None))
    return jax.shard_map(step, mesh=mesh, in_specs=in_specs, out_specs=P("grp", "blk"), check_vma=False)
```

time: 61.6 us -> 65.6 us (1.065)
  Pallas kernels: 57.4 us -> 63.8 us
  local copies, waits for them, and re-layouts: 3.87 us -> 1.57 us
    pallas_call x1, Pallas kernels: 57.4 us -> 63.8 us  [step(): pl.pallas_call(functools.partial(kernel, groups, blocks), out_shape=jax.S...]
    unnamed x7 -> x1, local copies, waits for them, and re-layouts: 3.17 us -> 1.57 us
    reshape x1 -> x0, local copies, waits for them, and re-layouts: 0.69 us -> none  [step(): weights.reshape(1, -1)]
where the time goes in v1:
time: 65.6 us; the launch traced here: 65.3 us
  Pallas kernels  63.8 us (97%)
  local copies, waits for them, and re-layouts  1.57 us (2%)
    pallas_call x1, Pallas kernels, step(): pl.pallas_call(functools.partial(kernel, groups, blocks), out_shape=jax.S...  63.8 us
    unnamed x1, local copies, waits for them, and re-layouts  1.57 us

profile of v1, /device:TPU:1, one launch (start us, length us, event | category | flops | bytes accessed | tf_op | source)
XLA Modules:
  0.0 65.3 jit_solution(4546014276919617771)
XLA Ops:
  0.0 63.8 %shard_map.46 = f32[16,2048]{1,0:T(8,128)} custom-call(f32[3,2048]{1,0:T(4,128)} %sens.1, bf16[3,2048]{1,0:T(4,128)(2,1)} %src.1, bf16[16,128]{1,0:T(8,128)(2,1)} %bitcast.1, bf16[2048,128]{1,0:T(8,128)(2,1)} %prb.1), custom_call_target="tpu_custom_call" | custom-call | tf_op jit(solution)/shard_map/pallas_call | solution.py:314
  63.8 1.6 %copy.6 = f32[16,2048]{1,0:T(8,128)} copy(f32[16,2048]{1,0:T(8,128)} %shard_map.46) | data formatting | bytes 262144

commit v2 on v1

v2 whole, which is shorter than its diff:
```python
import functools
import math

import jax
import jax.numpy as jnp
from jax import lax
from jax.experimental import pallas as pl
from jax.experimental.pallas import tpu as pltpu
from jax.sharding import PartitionSpec as P

STEPS = 6
EPS = 0.0025
BF, F32 = jnp.bfloat16, jnp.float32
MESH = pl.DeviceIdType.MESH

ORDER = ((0, 0, 1, 1, 2, 2, 5, 5, 4, 4, 3, 3), (1, 1, 2, 2, 6, 6, 5, 5, 4, 4, 3, 3))
TILE = 256
ON_MXU = 512


def pieces(v):
    hi = v.astype(BF).astype(F32)
    mid = (v - hi).astype(BF).astype(F32)
    return [hi, mid, v - hi - mid]


def squared(v):
    return v[0:1] * v[0:1] + v[1:2] * v[1:2] + v[2:3] * v[2:3]


def kernel(
    groups, blocks, sens, src, wgt, prb, out, own_sens, prb_in, src_in, wgt_in, prb_t, lhs, lanes, rhs, rows_of, ker_a, ker_b, sens_in, work,
    inbox, buf_a, buf_b, buf_c, buf_d, rcv, load, ready, sens_send, sens_recv, core_send, core_recv, a_send, a_recv, b_send, b_recv,
    c_send, c_recv, d_send, d_recv, f_send, f_recv,
):
    sources, sensors = src.shape[1], sens.shape[1]
    half, chunk = sensors // 2, sensors // 4
    nx = groups // 2
    grp, blk = lax.axis_index("grp"), lax.axis_index("blk")
    x, yh = grp // 2, grp % 2
    core = blk % 2
    other = grp + 1 - 2 * yh
    x_next = ((x + 1) % nx) * 2 + yh
    x_prev = ((x + nx - 1) % nx) * 2 + yh
    peer = blk + 1 - 2 * core

    def at(offset):
        return (blk + offset + blocks) % blocks

    def by_core(a, b):
        return a if a == b else jnp.where(core == 0, a, b)

    def signal(semaphore, device):
        pl.semaphore_signal(semaphore, inc=1, device_id=device, device_id_type=MESH)

    def copy(source, target, send, recv, device):
        return pltpu.make_async_remote_copy(source, target, send, recv, device_id=device, device_id_type=MESH)

    started = []

    def send(*args):
        started.append(copy(*args))
        started[-1].start()

    barrier = pltpu.get_barrier_semaphore()
    for o in range(1, STEPS):
        signal(barrier, (grp, at(-o)))
        pl.when(blk + o < blocks)(lambda o=o: signal(barrier, (grp, at(o))))
    for o in range(STEPS):
        signal(barrier, (other, at(-o)))
    for row in (x_next, x_prev):
        signal(barrier, (row, blk))
    expected = 3 * STEPS - jnp.maximum(STEPS - 1 - blk, 0)

    loads = [
        pltpu.make_async_copy(ref, target, load.at[i])
        for i, (ref, target) in enumerate(((src, src_in), (sens, own_sens), (wgt, wgt_in), (prb, prb_in)))
    ]
    for step in loads:
        step.start()
    rhs[...] = jnp.zeros_like(rhs)

    @pl.when(blk > blocks - STEPS)
    def _():
        pl.semaphore_wait(barrier, expected)
        for o in range(1, STEPS):
            pl.when(blk + o >= blocks)(lambda o=o: signal(ready.at[o - 1], (grp, at(o))))

    loads[0].wait()
    place = src_in[...].astype(F32)
    rows = [-2.0 * place] * 3 + [jnp.ones((3, sources), F32)] + pieces(squared(place)) + [jnp.zeros((113, sources), F32)]
    lhs[...] = jnp.transpose(jnp.concatenate(rows, axis=0)).astype(BF)
    if ON_MXU < chunk:
        for i in range(3):
            lanes[i] = jnp.transpose(jnp.broadcast_to(place[i : i + 1], (128, sources))).astype(BF)
    loads[1].wait()
    width = sensors // 8
    for r in range(8):
        span = slice(r * width, (r + 1) * width)
        sens_in[0, r : r + 1] = jnp.concatenate([own_sens[i : i + 1, span] for i in range(3)], axis=1)
    loads[2].wait()
    scale = 1.0 / math.sqrt(STEPS * sources * groups)
    weight = wgt_in[...].astype(F32) * scale
    weight = jnp.concatenate([weight[i : i + 1] for i in range(weight.shape[0])], axis=1)
    loads[3].wait()
    prb_t[...] = (jnp.transpose(prb_in[...]).astype(F32) * weight).astype(BF)

    def turn(hs):
        return by_core(ORDER[0][hs], ORDER[1][hs]), hs % 2

    def slot_of(hs):
        kk0, kk1 = ORDER[0][hs], ORDER[1][hs]
        j = hs % 2
        return by_core(j if kk0 == 0 else 2 * kk0 + 1 - j, j if kk1 == 6 else 2 * kk1 + 1 - j)

    def prepare(hs):
        kk, j = turn(hs)
        packed = sens_in[kk - core]
        packed = jnp.where(core == j, packed[4:8], packed[0:4])
        where = jnp.concatenate(
            [jnp.concatenate([packed[r : r + 1, i * width : (i + 1) * width] for r in range(4)], axis=1) for i in range(3)], axis=0
        )
        parts = pieces(where)
        rows = parts + pieces(squared(where) + EPS) + [jnp.ones((3, half), F32), jnp.zeros((1, half), F32)]
        rhs[hs % 2, 0:16] = jnp.concatenate(rows, axis=0).astype(BF)
        rows_of[hs % 2] = jnp.concatenate([parts[0], where - parts[0], jnp.zeros((2, half), F32)], axis=0)

    def evaluate(n, k):
        ker, hs, first = (ker_a, ker_b)[n % 2], n // 2, (n % 2) * chunk
        span = pl.ds(k * TILE, TILE)
        dist = jnp.dot(lhs[span], rhs[hs % 2, :, pl.ds(first, ON_MXU)], preferred_element_type=F32)
        ker[span, 0:ON_MXU] = lax.rsqrt(dist).astype(BF)
        width = chunk - ON_MXU
        if width == 0:
            return
        near = [
            jnp.broadcast_to(rows_of[hs % 2, i : i + 1, pl.ds(first + ON_MXU, width)], (16, width)).astype(BF) for i in range(6)
        ]
        for r in range(k * TILE, (k + 1) * TILE, 16):
            total = None
            for i in range(3):
                delta = jnp.concatenate([lanes[i, r : r + 16]] * (width // 128), axis=1) - near[i] - near[3 + i]
                total = delta * delta if total is None else total + delta * delta
            ker[r : r + 16, ON_MXU:chunk] = lax.rsqrt(total + jnp.asarray(EPS, BF))

    def block(n):
        part = None
        for k in range(sources // TILE):
            if n + 1 < 4 * STEPS:
                evaluate(n + 1, k)
            if n >= 0:
                span = pl.ds(k * TILE, TILE)
                term = jnp.dot(prb_t[:, span], (ker_a, ker_b)[n % 2][span], preferred_element_type=F32)
                part = term if part is None else part + term
        if n >= 0:
            part = part.astype(BF).reshape(groups, part.shape[0] // groups, chunk)
            work[slot_of(n // 2), n % 2] = part

    def unit_kk(u):
        return 6 * core if u < 2 else (1, 2, 5, 4, 3)[u - 2]

    def unit_at(u):
        return u if u < 2 else 2 * unit_kk(u)

    def unit_half(u):
        return core if u > 0 else 1 - core

    far, fore, back = (x + 2) % nx * 2, (x + 1) % nx * 2, (x + nx - 1) % nx * 2

    def to_peer(kk, c):
        s = kk - 1
        return copy(work.at[2 * kk + 1, c], inbox.at[s, c], core_send.at[s, c], core_recv.at[s, c], (grp, peer))

    def stage1(u, c):
        w = unit_at(u)
        if u >= 2:
            kk = unit_kk(u)
            to_peer(kk, c).wait_recv()
            work[w, c] = (work[w, c].astype(F32) + inbox[kk - 1, c].astype(F32)).astype(BF)
        send(work.at[w, c, far], buf_a.at[u, c], a_send.at[u, c], a_recv.at[u, c], (x_next, blk))
        send(work.at[w, c, far + 1], buf_b.at[u, c], b_send.at[u, c], b_recv.at[u, c], (x_prev, blk))

    def stage2(u, c):
        w = unit_at(u)
        copy(buf_a.at[u, c], buf_a.at[u, c], a_send.at[u, c], a_recv.at[u, c], (x_prev, blk)).wait_recv()
        work[w, c, fore] = (work[w, c, fore].astype(F32) + buf_a[u, c].astype(F32)).astype(BF)
        send(work.at[w, c, pl.ds(fore, 2)], buf_c.at[u, c], c_send.at[u, c], c_recv.at[u, c], (x_next, blk))
        copy(buf_b.at[u, c], buf_b.at[u, c], b_send.at[u, c], b_recv.at[u, c], (x_next, blk)).wait_recv()
        work[w, c, back + 1] = (work[w, c, back + 1].astype(F32) + buf_b[u, c].astype(F32)).astype(BF)
        send(work.at[w, c, pl.ds(back, 2)], buf_d.at[u, c], d_send.at[u, c], d_recv.at[u, c], (x_prev, blk))

    def final(u, c, away):
        w, kk, h = unit_at(u), unit_kk(u), unit_half(u)
        row = grp if away == 0 else other
        q = kk // 2
        return copy(work.at[w, c, row], rcv.at[q, away, h, c], f_send.at[u, c, away], f_recv.at[q, away, h, c], (row, at(kk - core)))

    holder = {0: 0, 1: 0, 2: 1}

    def stage3(u, c):
        w, h = unit_at(u), unit_half(u)
        copy(buf_c.at[u, c], buf_c.at[u, c], c_send.at[u, c], c_recv.at[u, c], (x_prev, blk)).wait_recv()
        copy(buf_d.at[u, c], buf_d.at[u, c], d_send.at[u, c], d_recv.at[u, c], (x_next, blk)).wait_recv()
        own = pl.ds(x * 2, 2)
        work[w, c, own] = (work[w, c, own].astype(F32) + buf_c[u, c].astype(F32) + buf_d[u, c].astype(F32)).astype(BF)
        final(u, c, 1).start()
        if u in holder:

            @pl.when(core == holder[u])
            def _():
                rcv[0, 0, h, c] = work[w, c, grp]

            @pl.when(core != holder[u])
            def _():
                final(u, c, 0).start()
        else:
            final(u, c, 0).start()

    def sensors_to(o):
        copy(sens_in.at[0], sens_in.at[o], sens_send.at[o - 1], sens_recv.at[o - 1], (grp, at(-o))).start()

    def sensors_late(o):
        pl.semaphore_wait(ready.at[o - 1], 1)
        sensors_to(o)

    def meet():
        with jax.named_scope("barrier_wait"):
            pl.when(blk <= blocks - STEPS)(lambda: pl.semaphore_wait(barrier, expected))
        for o in range(1, STEPS):
            pl.when(blk >= o)(lambda o=o: sensors_to(o))

    def scoped(name, action, *args):
        with jax.named_scope(name):
            action(*args)

    def late():
        for o in range(1, STEPS):
            pl.when(blk < o)(functools.partial(sensors_late, o))

    def arrived():
        for o in range(1, STEPS):
            copy(sens_in.at[0], sens_in.at[o], sens_send.at[o - 1], sens_recv.at[o - 1], (grp, at(o))).wait_recv()

    s1, s2, s3, both = "s1", "s2", "s3", (0, 1)
    does = {
        s1: stage1, s2: stage2, s3: stage3, "core": lambda kk, c: to_peer(kk, c).start(), "meet": meet, "late": late,
    }
    pair = lambda name, *units: [(name, u, c) for u in units for c in both]
    after = {
        0: [("meet",)],
        5: pair("core", 1),
        8: pair(s1, 2),
        9: pair("core", 2),
        11: pair(s1, 0, 1),
        12: pair(s1, 3) + pair(s2, 2),
        13: pair("core", 5),
        15: pair(s1, 4) + pair(s2, 0),
        16: pair(s2, 1, 3) + pair(s3, 2),
        17: pair("core", 4),
        19: pair(s1, 5) + pair(s2, 4) + pair(s3, 0),
        20: [("core", 3, 0)] + pair(s3, 1, 3),
        21: [("core", 3, 1)],
        22: [(s1, 6, 0)] + pair(s2, 5),
        23: [(s1, 6, 1)] + pair(s3, 4) + pair(s2, 6) + pair(s3, 5, 6),
    }
    after.setdefault(9, []).append(("late",))
    prepare(0)
    block(-1)
    for n in range(4 * STEPS):
        if n == 3:
            scoped("sens_wait", arrived)
        if n % 2 == 1 and n + 1 < 4 * STEPS:
            prepare((n + 1) // 2)
        block(n)
        for name, *args in after.get(n, ()):
            scoped("_".join([name, *map(str, args)]), does[name], *args)

    def landed(q, away, h):
        for c in both:
            slot = rcv.at[q, away, h, c]
            copy(slot, slot, f_send.at[0, 0, 0], f_recv.at[q, away, h, c], (other, blk)).wait_recv()

    def total(slots, h, c):
        base = None
        for q, away in slots:
            term = rcv[q, away, h, c].astype(F32)
            base = term if base is None else base + term
        return base

    def gather():
        pl.when(core == 1)(lambda: landed(0, 0, 0))
        for h in both:
            landed(0, 1, h)
            landed(2, 0, h)
            landed(2, 1, h)

            @pl.when(core == 0)
            def _(h=h):
                landed(3, 0, h)
                landed(3, 1, h)

            landed(1, 0, h)
            landed(1, 1, h)

    scoped("gather", gather)
    for h in both:
        for c in both:
            part = total([(q, away) for q in range(3) for away in both], h, c)
            far_part = total([(3, 0), (3, 1)], h, c)
            first = h * half + c * chunk
            out[:, first : first + chunk] = jnp.where(core == 0, part + far_part, part)

    for o in range(1, STEPS):
        copy(sens_in.at[0], sens_in.at[o], sens_send.at[o - 1], sens_recv.at[o - 1], (grp, at(-o))).wait_send()
    for kk in range(1, STEPS):
        for c in both:
            to_peer(kk, c).wait_send()
    for sent in started:
        sent.wait_send()
    for u in range(7):
        for c in both:
            final(u, c, 1).wait_send()
            if u in holder:
                pl.when(core != holder[u])(lambda u=u, c=c: final(u, c, 0).wait_send())
            else:
                final(u, c, 0).wait_send()


def solution(mesh):
    groups, blocks = mesh.shape["grp"], mesh.shape["blk"]

    def step(sensors, sources, weights, probes):
        (columns, probe), count = (sensors.shape[1], probes.shape[1]), probes.shape[0]
        rows, half, chunk = probe // groups, columns // 2, columns // 4
        dma = pltpu.SemaphoreType.DMA
        return pl.pallas_call(
            functools.partial(kernel, groups, blocks),
            out_shape=jax.ShapeDtypeStruct((rows, columns), F32),
            in_specs=[pl.BlockSpec(memory_space=pl.ANY)] * 4,
            out_specs=pl.BlockSpec(memory_space=pltpu.VMEM),
            scratch_shapes=[
                pltpu.VMEM((3, columns), F32),
                pltpu.VMEM((count, probe), BF),
                pltpu.VMEM((3, count), BF),
                pltpu.VMEM((count // 128, 128), BF),
                pltpu.VMEM((probe, count), BF),
                pltpu.VMEM((count, 128), BF),
                pltpu.VMEM((3, count if ON_MXU < chunk else 16, 128), BF),
                pltpu.VMEM((2, 128, half), BF),
                pltpu.VMEM((2, 8, half), F32),
                pltpu.VMEM((count, chunk), BF),
                pltpu.VMEM((count, chunk), BF),
                pltpu.VMEM((STEPS, 8, 3 * columns // 8), F32),
                pltpu.VMEM((12, 2, groups, rows, chunk), BF),
                pltpu.VMEM((5, 2, groups, rows, chunk), BF),
                pltpu.VMEM((7, 2, rows, chunk), BF),
                pltpu.VMEM((7, 2, rows, chunk), BF),
                pltpu.VMEM((7, 2, 2, rows, chunk), BF),
                pltpu.VMEM((7, 2, 2, rows, chunk), BF),
                pltpu.VMEM((4, 2, 2, 2, rows, chunk), BF),
                dma((4,)),
                pltpu.SemaphoreType.REGULAR((5,)),
                dma((5,)),
                dma((5,)),
                dma((5, 2)),
                dma((5, 2)),
            ]
            + [dma((7, 2))] * 8
            + [dma((7, 2, 2)), dma((4, 2, 2, 2))],
            compiler_params=pltpu.CompilerParams(collective_id=0, has_side_effects=True, vmem_limit_bytes=48 * 2**20),
        )(sensors, sources, weights.reshape(-1, 128), probes)

    in_specs = (P(None, "blk"), P(None, ("grp", "blk")), P(("grp", "blk")), P(("grp", "blk"), None))
    return jax.shard_map(step, mesh=mesh, in_specs=in_specs, out_specs=P("grp", "blk"), check_vma=False)
```

time: 65.6 us -> 67.2 us (1.024)
  local copies, waits for them, and re-layouts: 1.57 us -> 3.86 us
  Pallas kernels: 63.8 us -> 63 us
    unnamed x1 -> x9, local copies, waits for them, and re-layouts: 1.57 us -> 3.86 us
    pallas_call x1, Pallas kernels: 63.8 us -> 63 us  [step(): pl.pallas_call(functools.partial(kernel, groups, blocks), out_shape=jax.S...]
where the time goes in v2:
time: 67.2 us; the launch traced here: 66.9 us
  Pallas kernels  63 us (94%)
  local copies, waits for them, and re-layouts  3.86 us (6%)
    pallas_call x1, Pallas kernels, step(): pl.pallas_call(functools.partial(kernel, groups, blocks), out_shape=jax.S...  63 us
    unnamed x9, local copies, waits for them, and re-layouts  3.86 us

profile of v2, /device:TPU:1, one launch (start us, length us, event | category | flops | bytes accessed | tf_op | source)
XLA Modules:
  0.0 66.9 jit_solution(13071403092685039199)
XLA Ops:
  0.0 0.0 copy-start
  0.0 1.0 %copy-done = bf16[2048,128]{1,0:T(8,128)(2,1)S(1)} copy-done((bf16[2048,128]{1,0:T(8,128)(2,1)S(1)}, bf16[2048,128]{1,0:T(8,128)(2,1)}, u32[]{:S(2)}) %copy-start) | copy-done | bytes 524312
  1.0 0.0 copy-start.1
  1.0 0.8 %copy-done.1 = f32[3,2048]{1,0:T(4,128)S(1)} copy-done((f32[3,2048]{1,0:T(4,128)S(1)}, f32[3,2048]{1,0:T(4,128)}, u32[]{:S(2)}) %copy-start.1) | copy-done | bytes 24600
  1.8 0.0 copy-start.2
  1.8 0.7 %copy-done.2 = bf16[3,2048]{1,0:T(4,128)(2,1)S(1)} copy-done((bf16[3,2048]{1,0:T(4,128)(2,1)S(1)}, bf16[3,2048]{1,0:T(4,128)(2,1)}, u32[]{:S(2)}) %copy-start.2) | copy-done | bytes 12312
  2.5 0.0 copy-start.3
  2.5 0.7 %copy-done.3 = bf16[2048]{0:T(1024)(128)(2,1)S(1)} copy-done((bf16[2048]{0:T(1024)(128)(2,1)S(1)}, bf16[2048]{0:T(1024)(128)(2,1)}, u32[]{:S(2)}) %copy-start.3) | copy-done | bytes 4120
  3.2 63.0 %shard_map.46 = f32[16,2048]{1,0:T(8,128)S(1)} custom-call(f32[3,2048]{1,0:T(4,128)S(1)} %copy-done.1, bf16[3,2048]{1,0:T(4,128)(2,1)S(1)} %copy-done.2, bf16[16,128]{1,0:T(8,128)(2,1)S(1)} %bitcast.1, bf16[2048,128]{1,0:T(8,128)(2,1)S(1)} %copy-done), custom_call_target="tpu_custom_call" | custom-call | tf_op jit(solution)/shard_map/pallas_call | solution.py:336
  66.2 0.7 copy.6
Async XLA Ops:
  0.0 1.0 %copy-start = (bf16[2048,128]{1,0:T(8,128)(2,1)S(1)}, bf16[2048,128]{1,0:T(8,128)(2,1)}, u32[]{:S(2)}) copy-start(bf16[2048,128]{1,0:T(8,128)(2,1)} %prb.1) | copy-start | bytes 1572868
  1.0 0.8 %copy-start.1 = (f32[3,2048]{1,0:T(4,128)S(1)}, f32[3,2048]{1,0:T(4,128)}, u32[]{:S(2)}) copy-start(f32[3,2048]{1,0:T(4,128)} %sens.1) | copy-start | bytes 73732
  1.8 0.7 %copy-start.2 = (bf16[3,2048]{1,0:T(4,128)(2,1)S(1)}, bf16[3,2048]{1,0:T(4,128)(2,1)}, u32[]{:S(2)}) copy-start(bf16[3,2048]{1,0:T(4,128)(2,1)} %src.1) | copy-start | bytes 36868
  2.5 0.7 %copy-start.3 = (bf16[2048]{0:T(1024)(128)(2,1)S(1)}, bf16[2048]{0:T(1024)(128)(2,1)}, u32[]{:S(2)}) copy-start(bf16[2048]{0:T(1024)(128)(2,1)} %param.6) | copy-start | bytes 12292

commit v3 on v2

--- a/solution.py
+++ b/solution.py
@@ -14,6 +14,7 @@
 MESH = pl.DeviceIdType.MESH
 
 ORDER = ((0, 0, 1, 1, 2, 2, 5, 5, 4, 4, 3, 3), (1, 1, 2, 2, 6, 6, 5, 5, 4, 4, 3, 3))
+NEEDED = (1, 2, 5, 4, 3)
 TILE = 256
 ON_MXU = 512
 
@@ -226,7 +227,7 @@
     def meet():
         with jax.named_scope("barrier_wait"):
             pl.when(blk <= blocks - STEPS)(lambda: pl.semaphore_wait(barrier, expected))
-        for o in range(1, STEPS):
+        for o in NEEDED:
             pl.when(blk >= o)(lambda o=o: sensors_to(o))
 
     def scoped(name, action, *args):
@@ -234,12 +235,12 @@
             action(*args)
 
     def late():
-        for o in range(1, STEPS):
+        for o in NEEDED:
             pl.when(blk < o)(functools.partial(sensors_late, o))
 
-    def arrived():
-        for o in range(1, STEPS):
-            copy(sens_in.at[0], sens_in.at[o], sens_send.at[o - 1], sens_recv.at[o - 1], (grp, at(o))).wait_recv()
+    def arrived(hs):
+        t = turn(hs)[0] - core
+        copy(sens_in.at[0], sens_in.at[t], sens_send.at[t - 1], sens_recv.at[t - 1], (grp, at(t))).wait_recv()
 
     s1, s2, s3, both = "s1", "s2", "s3", (0, 1)
     does = {
@@ -263,13 +264,13 @@
         22: [(s1, 6, 0)] + pair(s2, 5),
         23: [(s1, 6, 1)] + pair(s3, 4) + pair(s2, 6) + pair(s3, 5, 6),
     }
-    after.setdefault(9, []).append(("late",))
+    after.setdefault(8, []).append(("late",))
     prepare(0)
     block(-1)
     for n in range(4 * STEPS):
-        if n == 3:
-            scoped("sens_wait", arrived)
         if n % 2 == 1 and n + 1 < 4 * STEPS:
+            if n % 4 == 3:
+                scoped(f"sens_wait_{n}", arrived, (n + 1) // 2)
             prepare((n + 1) // 2)
         block(n)
         for name, *args in after.get(n, ()):
@@ -336,7 +337,7 @@
         return pl.pallas_call(
             functools.partial(kernel, groups, blocks),
             out_shape=jax.ShapeDtypeStruct((rows, columns), F32),
-            in_specs=[pl.BlockSpec(memory_space=pl.ANY)] * 4,
+            in_specs=[pl.BlockSpec(memory_space=pltpu.HBM)] * 4,
             out_specs=pl.BlockSpec(memory_space=pltpu.VMEM),
             scratch_shapes=[
                 pltpu.VMEM((3, columns), F32),

time: 67.2 us -> 61.6 us (0.917)
  Pallas kernels: 63 us -> 57.5 us
    pallas_call x1, Pallas kernels: 63 us -> 57.5 us  [step(): pl.pallas_call(functools.partial(kernel, groups, blocks), out_shape=jax.S...]
where the time goes in v3:
time: 61.6 us; the launch traced here: 61.3 us
  Pallas kernels  57.5 us (93%)
  local copies, waits for them, and re-layouts  3.86 us (6%)
    pallas_call x1, Pallas kernels, step(): pl.pallas_call(functools.partial(kernel, groups, blocks), out_shape=jax.S...  57.5 us
    unnamed x9, local copies, waits for them, and re-layouts  3.86 us

profile of v3, /device:TPU:1, one launch (start us, length us, event | category | flops | bytes accessed | tf_op | source)
XLA Modules:
  0.0 61.3 jit_solution(16345126487278796321)
XLA Ops:
  0.0 0.0 copy-start
  0.0 1.0 %copy-done = bf16[2048,128]{1,0:T(8,128)(2,1)S(1)} copy-done((bf16[2048,128]{1,0:T(8,128)(2,1)S(1)}, bf16[2048,128]{1,0:T(8,128)(2,1)}, u32[]{:S(2)}) %copy-start) | copy-done | bytes 524312
  1.0 0.0 copy-start.1
  1.0 0.8 %copy-done.1 = f32[3,2048]{1,0:T(4,128)S(1)} copy-done((f32[3,2048]{1,0:T(4,128)S(1)}, f32[3,2048]{1,0:T(4,128)}, u32[]{:S(2)}) %copy-start.1) | copy-done | bytes 24600
  1.8 0.0 copy-start.2
  1.8 0.7 %copy-done.2 = bf16[3,2048]{1,0:T(4,128)(2,1)S(1)} copy-done((bf16[3,2048]{1,0:T(4,128)(2,1)S(1)}, bf16[3,2048]{1,0:T(4,128)(2,1)}, u32[]{:S(2)}) %copy-start.2) | copy-done | bytes 12312
  2.5 0.0 copy-start.3
  2.5 0.7 %copy-done.3 = bf16[2048]{0:T(1024)(128)(2,1)S(1)} copy-done((bf16[2048]{0:T(1024)(128)(2,1)S(1)}, bf16[2048]{0:T(1024)(128)(2,1)}, u32[]{:S(2)}) %copy-start.3) | copy-done | bytes 4120
  3.2 57.5 %shard_map.46 = f32[16,2048]{1,0:T(8,128)S(1)} custom-call(f32[3,2048]{1,0:T(4,128)S(1)} %copy-done.1, bf16[3,2048]{1,0:T(4,128)(2,1)S(1)} %copy-done.2, bf16[16,128]{1,0:T(8,128)(2,1)S(1)} %bitcast.1, bf16[2048,128]{1,0:T(8,128)(2,1)S(1)} %copy-done), custom_call_target="tpu_custom_call" | custom-call | tf_op jit(solution)/shard_map/pallas_call | solution.py:337
  60.7 0.7 %copy.6 = f32[16,2048]{1,0:T(8,128)} copy(f32[16,2048]{1,0:T(8,128)S(1)} %shard_map.46) | data formatting | bytes 262144
Async XLA Ops:
  0.0 1.0 %copy-start = (bf16[2048,128]{1,0:T(8,128)(2,1)S(1)}, bf16[2048,128]{1,0:T(8,128)(2,1)}, u32[]{:S(2)}) copy-start(bf16[2048,128]{1,0:T(8,128)(2,1)} %prb.1) | copy-start | bytes 1572868
  1.0 0.8 %copy-start.1 = (f32[3,2048]{1,0:T(4,128)S(1)}, f32[3,2048]{1,0:T(4,128)}, u32[]{:S(2)}) copy-start(f32[3,2048]{1,0:T(4,128)} %sens.1) | copy-start | bytes 73732
  1.8 0.7 %copy-start.2 = (bf16[3,2048]{1,0:T(4,128)(2,1)S(1)}, bf16[3,2048]{1,0:T(4,128)(2,1)}, u32[]{:S(2)}) copy-start(bf16[3,2048]{1,0:T(4,128)(2,1)} %src.1) | copy-start | bytes 36868
  2.5 0.7 %copy-start.3 = (bf16[2048]{0:T(1024)(128)(2,1)S(1)}, bf16[2048]{0:T(1024)(128)(2,1)}, u32[]{:S(2)}) copy-start(bf16[2048]{0:T(1024)(128)(2,1)} %param.6) | copy-start | bytes 12292

commit v4 on v3

--- a/solution.py
+++ b/solution.py
@@ -16,7 +16,7 @@
 ORDER = ((0, 0, 1, 1, 2, 2, 5, 5, 4, 4, 3, 3), (1, 1, 2, 2, 6, 6, 5, 5, 4, 4, 3, 3))
 NEEDED = (1, 2, 5, 4, 3)
 TILE = 256
-ON_MXU = 512
+ON_MXU = 256
 
 
 def pieces(v):
@@ -92,8 +92,11 @@
     rows = [-2.0 * place] * 3 + [jnp.ones((3, sources), F32)] + pieces(squared(place)) + [jnp.zeros((113, sources), F32)]
     lhs[...] = jnp.transpose(jnp.concatenate(rows, axis=0)).astype(BF)
     if ON_MXU < chunk:
+        row, column = (lax.broadcasted_iota(jnp.int32, (128, 384), d) for d in range(2))
+        spread = jnp.where(row == column // 128, -0.5, 0.0).astype(BF)
+        copies = jnp.dot(lhs[...], spread, preferred_element_type=F32).astype(BF)
         for i in range(3):
-            lanes[i] = jnp.transpose(jnp.broadcast_to(place[i : i + 1], (128, sources))).astype(BF)
+            lanes[i] = copies[:, i * 128 : (i + 1) * 128]
     loads[1].wait()
     width = sensors // 8
     for r in range(8):
@@ -250,21 +253,18 @@
     after = {
         0: [("meet",)],
         5: pair("core", 1),
-        8: pair(s1, 2),
-        9: pair("core", 2),
+        9: pair("core", 2) + pair(s1, 2),
         11: pair(s1, 0, 1),
-        12: pair(s1, 3) + pair(s2, 2),
-        13: pair("core", 5),
+        13: pair("core", 5) + pair(s1, 3) + pair(s2, 2),
         15: pair(s1, 4) + pair(s2, 0),
-        16: pair(s2, 1, 3) + pair(s3, 2),
-        17: pair("core", 4),
+        17: pair("core", 4) + pair(s2, 1, 3) + pair(s3, 2),
         19: pair(s1, 5) + pair(s2, 4) + pair(s3, 0),
         20: [("core", 3, 0)] + pair(s3, 1, 3),
         21: [("core", 3, 1)],
         22: [(s1, 6, 0)] + pair(s2, 5),
         23: [(s1, 6, 1)] + pair(s3, 4) + pair(s2, 6) + pair(s3, 5, 6),
     }
-    after.setdefault(8, []).append(("late",))
+    after.setdefault(9, []).append(("late",))
     prepare(0)
     block(-1)
     for n in range(4 * STEPS):
@@ -368,7 +368,7 @@
             ]
             + [dma((7, 2))] * 8
             + [dma((7, 2, 2)), dma((4, 2, 2, 2))],
-            compiler_params=pltpu.CompilerParams(collective_id=0, has_side_effects=True, vmem_limit_bytes=48 * 2**20),
+            compiler_params=pltpu.CompilerParams(collective_id=0, has_side_effects=True, vmem_limit_bytes=63500000),
         )(sensors, sources, weights.reshape(-1, 128), probes)
 
     in_specs = (P(None, "blk"), P(None, ("grp", "blk")), P(("grp", "blk")), P(("grp", "blk"), None))

time: 61.6 us -> 60.9 us (0.989)
  local copies, waits for them, and re-layouts: 3.86 us -> 1.57 us
  Pallas kernels: 57.5 us -> 59.2 us
    unnamed x9 -> x1, local copies, waits for them, and re-layouts: 3.86 us -> 1.57 us
    pallas_call x1, Pallas kernels: 57.5 us -> 59.2 us  [step(): pl.pallas_call(functools.partial(kernel, groups, blocks), out_shape=jax.S...]
where the time goes in v4:
time: 60.9 us; the launch traced here: 60.8 us
  Pallas kernels  59.2 us (97%)
  local copies, waits for them, and re-layouts  1.57 us (3%)
    pallas_call x1, Pallas kernels, step(): pl.pallas_call(functools.partial(kernel, groups, blocks), out_shape=jax.S...  59.2 us
    unnamed x1, local copies, waits for them, and re-layouts  1.57 us

profile of v4, /device:TPU:1, one launch (start us, length us, event | category | flops | bytes accessed | tf_op | source)
XLA Modules:
  0.0 60.8 jit_solution(11657616079229729823)
XLA Ops:
  0.0 59.2 %shard_map.46 = f32[16,2048]{1,0:T(8,128)} custom-call(f32[3,2048]{1,0:T(4,128)} %sens.1, bf16[3,2048]{1,0:T(4,128)(2,1)} %src.1, bf16[16,128]{1,0:T(8,128)(2,1)} %bitcast.1, bf16[2048,128]{1,0:T(8,128)(2,1)} %prb.1), custom_call_target="tpu_custom_call" | custom-call | tf_op jit(solution)/shard_map/pallas_call | solution.py:337
  59.2 1.6 %copy.6 = f32[16,2048]{1,0:T(8,128)} copy(f32[16,2048]{1,0:T(8,128)} %shard_map.46) | data formatting | bytes 262144

commit v5 on v4

--- a/solution.py
+++ b/solution.py
@@ -81,12 +81,6 @@
         step.start()
     rhs[...] = jnp.zeros_like(rhs)
 
-    @pl.when(blk > blocks - STEPS)
-    def _():
-        pl.semaphore_wait(barrier, expected)
-        for o in range(1, STEPS):
-            pl.when(blk + o >= blocks)(lambda o=o: signal(ready.at[o - 1], (grp, at(o))))
-
     loads[0].wait()
     place = src_in[...].astype(F32)
     rows = [-2.0 * place] * 3 + [jnp.ones((3, sources), F32)] + pieces(squared(place)) + [jnp.zeros((113, sources), F32)]
@@ -97,6 +91,12 @@
         copies = jnp.dot(lhs[...], spread, preferred_element_type=F32).astype(BF)
         for i in range(3):
             lanes[i] = copies[:, i * 128 : (i + 1) * 128]
+    @pl.when(blk > blocks - STEPS)
+    def _():
+        pl.semaphore_wait(barrier, expected)
+        for o in range(1, STEPS):
+            pl.when(blk + o >= blocks)(lambda o=o: signal(ready.at[o - 1], (grp, at(o))))
+
     loads[1].wait()
     width = sensors // 8
     for r in range(8):
@@ -264,7 +264,7 @@
         22: [(s1, 6, 0)] + pair(s2, 5),
         23: [(s1, 6, 1)] + pair(s3, 4) + pair(s2, 6) + pair(s3, 5, 6),
     }
-    after.setdefault(9, []).append(("late",))
+    after.setdefault(7, []).append(("late",))
     prepare(0)
     block(-1)
     for n in range(4 * STEPS):
@@ -303,6 +303,23 @@
             landed(1, 0, h)
             landed(1, 1, h)
 
+    def finish(*units):
+        for u in units:
+            for c in both:
+                final(u, c, 1).wait_send()
+                if u in holder:
+                    pl.when(core != holder[u])(lambda u=u, c=c: final(u, c, 0).wait_send())
+                else:
+                    final(u, c, 0).wait_send()
+
+    for o in range(1, STEPS):
+        copy(sens_in.at[0], sens_in.at[o], sens_send.at[o - 1], sens_recv.at[o - 1], (grp, at(-o))).wait_send()
+    for kk in range(1, STEPS):
+        for c in both:
+            to_peer(kk, c).wait_send()
+    for sent in started:
+        sent.wait_send()
+    finish(0, 1, 2, 3, 4)
     scoped("gather", gather)
     for h in both:
         for c in both:
@@ -311,20 +328,7 @@
             first = h * half + c * chunk
             out[:, first : first + chunk] = jnp.where(core == 0, part + far_part, part)
 
-    for o in range(1, STEPS):
-        copy(sens_in.at[0], sens_in.at[o], sens_send.at[o - 1], sens_recv.at[o - 1], (grp, at(-o))).wait_send()
-    for kk in range(1, STEPS):
-        for c in both:
-            to_peer(kk, c).wait_send()
-    for sent in started:
-        sent.wait_send()
-    for u in range(7):
-        for c in both:
-            final(u, c, 1).wait_send()
-            if u in holder:
-                pl.when(core != holder[u])(lambda u=u, c=c: final(u, c, 0).wait_send())
-            else:
-                final(u, c, 0).wait_send()
+    finish(5, 6)
 
 
 def solution(mesh):

time: 60.9 us -> 60.4 us (level)
  no operation moved by 1% of the time
where the time goes in v5:
time: 60.4 us; the launch traced here: 60.2 us
  Pallas kernels  58.6 us (97%)
  local copies, waits for them, and re-layouts  1.57 us (3%)
    pallas_call x1, Pallas kernels, step(): pl.pallas_call(functools.partial(kernel, groups, blocks), out_shape=jax.S...  58.6 us
    unnamed x1, local copies, waits for them, and re-layouts  1.57 us

profile of v5, /device:TPU:1, one launch (start us, length us, event | category | flops | bytes accessed | tf_op | source)
XLA Modules:
  0.0 60.2 jit_solution(14024093094549242135)
XLA Ops:
  0.0 58.6 %shard_map.46 = f32[16,2048]{1,0:T(8,128)} custom-call(f32[3,2048]{1,0:T(4,128)} %sens.1, bf16[3,2048]{1,0:T(4,128)(2,1)} %src.1, bf16[16,128]{1,0:T(8,128)(2,1)} %bitcast.1, bf16[2048,128]{1,0:T(8,128)(2,1)} %prb.1), custom_call_target="tpu_custom_call" | custom-call | tf_op jit(solution)/shard_map/pallas_call | solution.py:341
  58.6 1.6 %copy.6 = f32[16,2048]{1,0:T(8,128)} copy(f32[16,2048]{1,0:T(8,128)} %shard_map.46) | data formatting | bytes 262144
